TPU v7x, 32 devices: a whole 2x2x4 slice. The times are simulated.
32 devices in a mesh: group: 2 (over y), expert: 4 (over x, core), tensor: 4 (over z).
Axes of the slice: x: 2, y: 2, z: 4, core: 2. Of those that a mesh axis runs over, the one named last changes fastest.
Arguments:
- tokens: bfloat16 [512, 4096], P(('group', 'expert'), 'tensor'), parts along dimension 0, may hold values from -6 to 6
- w_gate: bfloat16 [8, 4096, 1536], P('expert', 'tensor'), may hold values from -0.125 to 0.125
- w_up: bfloat16 [8, 4096, 1536], P('expert', 'tensor'), may hold values from -0.125 to 0.125
- w_down: bfloat16 [8, 1536, 4096], P('expert', None, 'tensor'), may hold values from -0.15625 to 0.15625
- expert_ids: int32 [512, 8], P(('group', 'expert')), parts along dimension 0, may hold values from 0 to 7, as said below
- route_weights: float32 [512, 8], P(('group', 'expert')), parts along dimension 0, may hold values from 0.05 to 0.5
Outputs:
- mixed_out: bfloat16 [512, 4096], P(('group', 'expert'), 'tensor'), parts along dimension 0
There are 2 independent parts, one for each index of `group`. A program takes and returns all parts, laid end to end along the dimension named above; an argument that names none is the same for every part. Nothing has to cross between parts.
Inputs may be any that keep to these rules, and one draw needn't show every extreme that they name: `expert_ids`: each row names 8 different experts. In each aligned block of 64 rows no expert is named by more than 64 rows, and one expert, the same in every block of a part, is named by exactly 64 rows of every block.
All inputs are finite; a program needn't handle non-finite values.
Results may differ from a plain program's by a relative error of at most 0.0057.
Values may be sent and summed in bfloat16 or wider, within the bound.
A program may use at most 128 MiB of HBM per device.

v0:
```python
import jax
import jax.numpy as jnp
from jax import lax
from jax.sharding import PartitionSpec as P


def slot_numbers(flat_ids, experts_all):
    labels = jnp.arange(experts_all, dtype=jnp.int32)
    onehot = (flat_ids[:, None] == labels[None, :]).astype(jnp.int32)
    before = jnp.cumsum(onehot, axis=0) - onehot
    return jnp.sum(before * onehot, axis=1)


def per_device(tokens, w_gate, w_up, w_down, expert_ids, route_weights):
    n_expert = lax.axis_size("expert")
    held_experts = w_gate.shape[0]
    experts_all = held_experts * n_expert
    tok_rows = tokens.shape[0]
    col_share = tokens.shape[1]
    per_token = expert_ids.shape[1]
    capacity = min(tok_rows, 2 * tok_rows * per_token // experts_all)
    flat_ids = expert_ids.reshape(tok_rows * per_token)
    position = flat_ids * capacity + slot_numbers(flat_ids, experts_all)
    owners = jnp.arange(tok_rows * per_token, dtype=jnp.int32) // per_token
    source = jnp.full((experts_all * capacity,), -1, jnp.int32).at[position].set(owners)
    filled = (source >= 0)[:, None]
    picked_rows = jnp.where(filled, tokens[jnp.maximum(source, 0)], jnp.zeros((), tokens.dtype))
    outgoing = picked_rows.reshape(n_expert, held_experts, capacity, col_share)
    received = lax.all_to_all(outgoing, "expert", split_axis=0, concat_axis=0, tiled=True)
    gate_part = jnp.einsum("sjnd,jdf->sjnf", received, w_gate, preferred_element_type=jnp.float32)
    up_part = jnp.einsum("sjnd,jdf->sjnf", received, w_up, preferred_element_type=jnp.float32)
    gate_share = lax.psum_scatter(gate_part, "tensor", scatter_dimension=3, tiled=True)
    up_share = lax.psum_scatter(up_part, "tensor", scatter_dimension=3, tiled=True)
    hidden_share = (jax.nn.silu(gate_share) * up_share).astype(jnp.bfloat16)
    hidden = lax.all_gather(hidden_share, "tensor", axis=3, tiled=True)
    result = jnp.einsum("sjnf,jfd->sjnd", hidden, w_down, preferred_element_type=jnp.float32)
    returned = result.astype(jnp.bfloat16)
    combined = lax.all_to_all(returned, "expert", split_axis=0, concat_axis=0, tiled=True).reshape(
        experts_all * capacity, col_share
    )
    picked = combined[position].reshape(tok_rows, per_token, col_share).astype(jnp.float32)
    mixed_out = jnp.sum(picked * route_weights[:, :, None], axis=1)
    return mixed_out.astype(jnp.bfloat16)


def solution(mesh):
    in_specs = (
        P(("group", "expert"), "tensor"),
        P("expert", "tensor", None),
        P("expert", "tensor", None),
        P("expert", None, "tensor"),
        P(("group", "expert"), None),
        P(("group", "expert"), None),
    )
    out_specs = P(("group", "expert"), "tensor")
    return jax.shard_map(
        per_device, mesh=mesh, in_specs=in_specs, out_specs=out_specs, check_vma=False
    )
```

profile of v0, /device:TPU:0, one launch (start us, length us, event | category | flops | bytes accessed | tf_op | source)
XLA Modules:
  0.0 236.0 jit_solution(6427868677075579159)
XLA Ops:
  6.5 0.0 copy-start
  6.5 0.0 reduce-scatter.3.cloned.1.call-start
  6.5 0.8 copy.16
  7.3 0.1 eq.29
  7.4 0.1 eq.25
  7.5 0.7 broadcast_multiply_fusion
  8.2 1.1 reduce-window.6
  9.4 0.2 slice_reduce_fusion
  9.6 0.1 copy.15
  9.7 0.1 mul.32
  9.8 0.1 fusion.22
  9.9 2.4 %scatter_custom_fusion = s32[512]{0:T(512)S(1)} fusion(s32[512]{0:T(512)S(1)} %bitcast.47, s32[512]{0:T(512)S(1)} %add_select_fusion, s32[]{:T(128)} %constant.27.clone.1), kind=kCustom, calls=%fused_computation.39 | custom fusion | bytes 2052 | tf_op jit(solution)/shard_map/scatter | solution.py:25
  12.4 0.1 broadcast_in_dim.26
  12.5 0.0 copy-done
  12.5 2.1 gather_fusion
  14.5 0.1 broadcast_select_fusion
  14.7 18.5 %all_to_all.10 = bf16[4,2,64,1024]{3,2,1,0:T(8,128)(2,1)S(1)} all-to-all(bf16[4,2,64,1024]{3,2,1,0:T(8,128)(2,1)S(1)} %broadcast_select_fusion), channel_id=1, replica_groups=mesh['group'=2,'expert'=4,'tensor'=4] {'expert'}, dimensions={0} | all-to-all | bytes 2097152 | tf_op jit(solution)/shard_map/all_to_all | solution.py:29
  33.2 6.3 %fusion.6 = f32[4,2,64,1536]{3,2,0,1:T(8,128)} fusion(bf16[2,1024,1536]{2,1,0:T(8,128)(2,1)} %param.7, bf16[4,2,64,1024]{3,2,1,0:T(8,128)(2,1)S(1)} %all_to_all.10), kind=kOutput, calls=%fused_computation.9 | convolution fusion | flops 1610612736 | bytes 10485760 | tf_op jit(solution)/shard_map/sjnd,jdf->sjnf/dot_general | solution.py:30
  39.4 0.0 reduce-scatter.3.cloned.1.call-update
  39.5 0.0 reduce-scatter.5.cloned.1.call-start
  39.5 6.3 %fusion.9 = f32[4,2,64,1536]{3,2,0,1:T(8,128)} fusion(bf16[2,1024,1536]{2,1,0:T(8,128)(2,1)} %param.8, bf16[4,2,64,1024]{3,2,1,0:T(8,128)(2,1)S(1)} %all_to_all.10), kind=kOutput, calls=%fused_computation.10 | convolution fusion | flops 1610612736 | bytes 10485760 | tf_op jit(solution)/shard_map/sjnd,jdf->sjnf/dot_general | solution.py:31
  45.8 0.0 reduce-scatter.5.cloned.1.call-update
  45.8 0.0 all-gather.2.cloned.1.call-start
  45.9 54.4 %reduce-scatter.3.cloned.1.call-done = f32[4,2,64,384]{3,2,0,1:T(8,128)} async-done(((f32[4,2,64,1536]{3,2,0,1:T(8,128)}), f32[4,2,64,384]{3,2,0,1:T(8,128)}) %reduce-scatter.3.cloned.1.call-update) | async-done | bytes 786448 | tf_op jit(solution)/shard_map/reduce_scatter | solution.py:32
  100.3 62.6 %reduce-scatter.5.cloned.1.call-done = f32[4,2,64,384]{3,2,0,1:T(8,128)} async-done(((f32[4,2,64,1536]{3,2,0,1:T(8,128)}), f32[4,2,64,384]{3,2,0,1:T(8,128)}) %reduce-scatter.5.cloned.1.call-update) | async-done | bytes 786448 | tf_op jit(solution)/shard_map/reduce_scatter | solution.py:33
  163.0 2.3 multiply_convert_fusion
  165.3 0.0 all-gather.2.cloned.1.call-update
  165.3 0.0 copy-start.1
  165.3 36.7 %all-gather.2.cloned.1.call-done = bf16[4,2,64,1536]{3,2,0,1:T(8,128)(2,1)} async-done(((bf16[4,2,64,384]{3,2,0,1:T(8,128)(2,1)}), bf16[4,2,64,1536]{3,2,0,1:T(8,128)(2,1)}) %all-gather.2.cloned.1.call-update) | async-done | bytes 1572880 | tf_op jit(solution)/shard_map/all_gather | solution.py:35
  202.0 5.1 %fusion.16 = bf16[4,2,64,1024]{3,2,0,1:T(8,128)(2,1)S(1)} fusion(bf16[4,2,64,1536]{3,2,0,1:T(8,128)(2,1)} %all-gather.2.cloned.1.call-done, bf16[2,1536,1024]{2,1,0:T(8,128)(2,1)} %param.9), kind=kOutput, calls=%fused_computation.14 | convolution fusion | flops 1611137024 | bytes 8912896 | tf_op jit(solution)/shard_map/sjnf,jfd->sjnd/dot_general | solution.py:36
  207.1 1.1 copy.20
  208.1 3.5 %all-to-all-start.1 = ((bf16[4,2,64,1024]{3,2,1,0:T(8,128)(2,1)}), bf16[4,2,64,1024]{3,2,1,0:T(8,128)(2,1)S(1)}, u32[]{:S(2)}, u32[]{:S(2)}) async-start(bf16[4,2,64,1024]{3,2,1,0:T(8,128)(2,1)} %copy.20), calls=%async_computation.3 | async-start | bytes 2097152 | tf_op jit(solution)/shard_map/all_to_all | solution.py:38
  211.7 0.0 copy-done.1
  211.7 0.1 copy.21
  211.8 14.3 %all-to-all-done.1 = bf16[4,2,64,1024]{3,2,1,0:T(8,128)(2,1)S(1)} async-done(((bf16[4,2,64,1024]{3,2,1,0:T(8,128)(2,1)}), bf16[4,2,64,1024]{3,2,1,0:T(8,128)(2,1)S(1)}, u32[]{:S(2)}, u32[]{:S(2)}) %all-to-all-start.1) | async-done | bytes 1048608 | tf_op jit(solution)/shard_map/all_to_all | solution.py:38
  226.1 2.0 gather_fusion.1
  228.1 1.4 fusion.12
  (9 shorter events, 0.1 us)
Async XLA Ops:
  6.5 6.0 %copy-start = (bf16[64,1024]{1,0:T(8,128)(2,1)S(1)}, bf16[64,1024]{1,0:T(8,128)(2,1)}, u32[]{:S(2)}) copy-start(bf16[64,1024]{1,0:T(8,128)(2,1)} %param.6) | copy-start | bytes 393220
  6.5 93.8 %reduce-scatter.3.cloned.1.call-start = ((), (), s32[]{:S(2)}) async-start(), calls=%async_computation.4 | async-start | bytes 3932160 | tf_op jit(solution)/shard_map/reduce_scatter | solution.py:32
  39.5 123.5 %reduce-scatter.5.cloned.1.call-start = ((), (), s32[]{:S(2)}) async-start(), calls=%async_computation.5 | async-start | bytes 3932160 | tf_op jit(solution)/shard_map/reduce_scatter | solution.py:33
  45.8 156.2 %all-gather.2.cloned.1.call-start = ((), (), s32[]{:S(2)}) async-start(), calls=%async_computation.6 | async-start | bytes 1966080 | tf_op jit(solution)/shard_map/all_gather | solution.py:35
  165.3 46.3 %copy-start.1 = (f32[64,8]{0,1:T(8,128)S(1)}, f32[64,8]{0,1:T(8,128)}, u32[]{:S(2)}) copy-start(f32[64,8]{0,1:T(8,128)} %param.11) | copy-start | bytes 6148
  208.1 17.9 %all-to-all-start.1 = ((bf16[4,2,64,1024]{3,2,1,0:T(8,128)(2,1)}), bf16[4,2,64,1024]{3,2,1,0:T(8,128)(2,1)S(1)}, u32[]{:S(2)}, u32[]{:S(2)}) async-start(bf16[4,2,64,1024]{3,2,1,0:T(8,128)(2,1)} %copy.20), calls=%async_computation.3 | async-start | bytes 2097152 | tf_op jit(solution)/shard_map/all_to_all | solution.py:38
Sparse Core Ops, SparseCore 0:
  39.6 60.6 reduce-scatter.2
  102.6 60.3 reduce-scatter.4
  165.4 36.5 all-gather.1
where the time goes:
time: 236 us
  waiting for transfers between devices  168 us (71%)
  blocking collectives  18.5 us (8%)
  matrix products  17.6 us (7%)
  between operations  13.2 us (6%)
  local copies, waits for them, and re-layouts  9.18 us (4%)
  other arithmetic  5.83 us (2%)
  starting transfers between devices  3.6 us (2%)
    reduce_scatter x1, waiting for transfers between devices, per_device(): lax.psum_scatter(up_part, 'tensor', scatter_dimension=3, tiled=True)  62.6 us
    reduce_scatter x1, waiting for transfers between devices, per_device(): lax.psum_scatter(gate_part, 'tensor', scatter_dimension=3, tiled=True)  54.4 us
    all_gather x1, waiting for transfers between devices, per_device(): hidden = lax.all_gather(hidden_share, 'tensor', axis=3, tiled=True)  36.7 us
    all_to_all x1, blocking collectives, per_device(): lax.all_to_all(outgoing, 'expert', split_axis=0, concat_axis=0, tiled=True)  18.5 us
    all_to_all x1, waiting for transfers between devices, per_device(): lax.all_to_all(returned, 'expert', split_axis=0, concat_axis=0, tiled=True)  14.3 us
    dot_general x1, matrix products, per_device(): jnp.einsum('sjnd,jdf->sjnf', received, w_up, preferred_element_type=jnp.f...  6.3 us
    dot_general x1, matrix products, per_device(): jnp.einsum('sjnd,jdf->sjnf', received, w_gate, preferred_element_type=jnp...  6.27 us
    dot_general x1, matrix products, per_device(): jnp.einsum('sjnf,jfd->sjnd', hidden, w_down, preferred_element_type=jnp.f...  5.06 us
  transfers between devices with their start and end apart: 4, of which 4 were waited for; matrix products, arithmetic and copies ran while one was open for 3% of the time, Pallas kernels for 0%

commit v1 on v0

--- a/solution.py
+++ b/solution.py
@@ -1,6 +1,10 @@
+import functools
+
 import jax
 import jax.numpy as jnp
 from jax import lax
+from jax.experimental import pallas as pl
+from jax.experimental.pallas import tpu as pltpu
 from jax.sharding import PartitionSpec as P
 
 
@@ -11,7 +15,7 @@
     return jnp.sum(before * onehot, axis=1)
 
 
-def per_device(tokens, w_gate, w_up, w_down, expert_ids, route_weights):
+def routed_by_slots(tokens, w_gate, w_up, w_down, expert_ids, route_weights):
     n_expert = lax.axis_size("expert")
     held_experts = w_gate.shape[0]
     experts_all = held_experts * n_expert
@@ -43,6 +47,255 @@
     return mixed_out.astype(jnp.bfloat16)
 
 
+LANES = 128
+RS_LAG = 2
+AG_LAG = 2
+OUT_CHUNKS = 4
+MESH = pl.DeviceIdType.MESH
+
+
+def layer_kernel(
+    n_expert, n_tensor, tok_ref, route_ref, wg_hbm, wu_hbm, wd_hbm, out_ref,
+    rows_ref, routes_ref, scale_ref, wg_ref, wu_ref, wd_ref, part_ref, sent_ref, got_ref, hidden_ref,
+    own_ref, ret_out_ref, ret_in_ref,
+    w_sem, tok_send, tok_recv, route_send, route_recv, rs_send, rs_recv, ag_send, ag_recv, ret_send, ret_recv,
+):
+    held, depth, ff = wg_ref.shape
+    tok_rows, cols = tok_ref.shape
+    all_rows = n_expert * tok_rows
+    per_expert = ff // LANES
+    items = held * per_expert // 2
+    me = lax.axis_index("expert")
+    at = lax.axis_index("tensor")
+    last = n_tensor - 1
+    peers = [lax.rem(me + k, n_expert) for k in range(1, n_expert)]
+
+    loads = []
+    for j in range(held):
+        for k, (hbm, vmem) in enumerate(((wg_hbm, wg_ref), (wu_hbm, wu_ref))):
+            loads.append(pltpu.make_async_copy(hbm.at[j], vmem.at[j], w_sem.at[2 * j + k]))
+    loads.append(pltpu.make_async_copy(wd_hbm, wd_ref, w_sem.at[2 * held]))
+    for load in loads:
+        load.start()
+
+    barrier = pltpu.get_barrier_semaphore()
+    for peer in peers:
+        pl.semaphore_signal(barrier, inc=1, device_id={"expert": peer}, device_id_type=MESH)
+
+    @pl.when(at > 0)
+    def _():
+        pl.semaphore_signal(barrier, inc=1, device_id={"tensor": at - 1}, device_id_type=MESH)
+
+    @pl.when(at < last)
+    def _():
+        pl.semaphore_signal(barrier, inc=1, device_id={"tensor": at + 1}, device_id_type=MESH)
+
+    greeted = (n_expert - 1) + (at > 0).astype(jnp.int32) + (at < last).astype(jnp.int32)
+    pl.semaphore_wait(barrier, greeted)
+
+    def tok_copy(k, slot):
+        return pltpu.make_async_remote_copy(
+            src_ref=tok_ref, dst_ref=rows_ref.at[slot], send_sem=tok_send.at[k], recv_sem=tok_recv.at[slot],
+            device_id={"expert": peers[k]}, device_id_type=MESH)
+
+    def route_copy(k, slot):
+        return pltpu.make_async_remote_copy(
+            src_ref=route_ref, dst_ref=routes_ref.at[slot], send_sem=route_send.at[k], recv_sem=route_recv.at[slot],
+            device_id={"expert": peers[k]}, device_id_type=MESH)
+
+    for k in range(n_expert - 1):
+        tok_copy(k, me).start()
+    for k in range(n_expert - 1):
+        route_copy(k, me).start()
+    rows_ref[me] = tok_ref[...]
+    routes_ref[me] = route_ref[...]
+    for load in loads[:-1]:
+        load.wait()
+    for k in range(n_expert - 1):
+        tok_copy(k, peers[k]).wait_recv()
+    for k in range(n_expert - 1):
+        route_copy(k, peers[k]).wait_recv()
+    routes = routes_ref[...].reshape(all_rows, LANES)
+    lane = lax.broadcasted_iota(jnp.int32, (all_rows, LANES), 1)
+    for j in range(held):
+        mine = jnp.sum(jnp.where(lane == me * held + j, routes, 0.0), axis=1, keepdims=True)
+        scale_ref[j] = jnp.broadcast_to(mine, (all_rows, LANES))
+
+    far = (last - at, at)
+    onward = (jnp.maximum(at - 1, 0), jnp.minimum(at + 1, last))
+    back = (jnp.minimum(at + 1, last), jnp.maximum(at - 1, 0))
+
+    def rs_copy(f, i):
+        return pltpu.make_async_remote_copy(
+            src_ref=sent_ref.at[f, i], dst_ref=got_ref.at[f, i], send_sem=rs_send.at[f, i], recv_sem=rs_recv.at[f, i],
+            device_id={"tensor": onward[f]}, device_id_type=MESH)
+
+    def ag_copy(f, i):
+        return pltpu.make_async_remote_copy(
+            src_ref=hidden_ref.at[f, i], dst_ref=hidden_ref.at[f, i], send_sem=ag_send.at[f, i],
+            recv_sem=ag_recv.at[f, i], device_id={"tensor": back[f]}, device_id_type=MESH)
+
+    def compute_part(f, i):
+        q = f * items + i
+        j = q // per_expert
+        start = pl.multiple_of(lax.rem(q, per_expert) * LANES, LANES)
+        both = jnp.concatenate([wg_ref[j, :, pl.ds(start, LANES)], wu_ref[j, :, pl.ds(start, LANES)]], axis=1)
+        part_ref[f] = jnp.dot(rows_ref[...].reshape(all_rows, depth), both, preferred_element_type=jnp.float32)
+
+    def finish_part(f, i):
+        @pl.when(far[f] > 0)
+        def _():
+            rs_copy(f, i).wait_recv()
+            part_ref[f] = part_ref[f] + got_ref[f, i].astype(jnp.float32)
+
+        @pl.when(far[f] < last)
+        def _():
+            sent_ref[f, i] = part_ref[f].astype(jnp.bfloat16)
+            rs_copy(f, i).start()
+
+        @pl.when(far[f] == last)
+        def _():
+            gate = part_ref[f, :, :LANES]
+            up = part_ref[f, :, LANES:]
+            j = (f * items + i) // per_expert
+            hidden_ref[f, i] = (jax.nn.silu(gate) * up * scale_ref[j]).astype(jnp.bfloat16)
+            ag_copy(f, i).start()
+
+    def forward(f, i):
+        ag_copy(f, i).wait_recv()
+
+        @pl.when(far[f] > 0)
+        def _():
+            ag_copy(f, i).start()
+
+    def step(s, carry):
+        for f in range(2):
+            i = s - RS_LAG * far[f]
+
+            @pl.when((i >= 0) & (i < items))
+            def _():
+                compute_part(f, i)
+
+        for f in range(2):
+            h = s - RS_LAG * last - AG_LAG * (last - far[f])
+
+            @pl.when((h >= 0) & (h < items) & (far[f] < last))
+            def _():
+                forward(f, h)
+
+            i = s - RS_LAG * far[f]
+
+            @pl.when((i >= 0) & (i < items))
+            def _():
+                finish_part(f, i)
+
+        return carry
+
+    lax.fori_loop(0, items + (RS_LAG + AG_LAG) * last, step, 0)
+
+    loads[-1].wait()
+
+    def ret_copy(c, k, target, source):
+        return pltpu.make_async_remote_copy(
+            src_ref=ret_out_ref.at[c, target], dst_ref=ret_in_ref.at[c, source],
+            send_sem=ret_send.at[c, k], recv_sem=ret_recv.at[c, source],
+            device_id={"expert": peers[k]}, device_id_type=MESH)
+
+    width = cols // OUT_CHUNKS
+    mixed_in = jnp.concatenate([hidden_ref[f, i] for f in range(2) for i in range(items)], axis=1)
+    for c in range(OUT_CHUNKS):
+        down = wd_ref[:, :, c * width:(c + 1) * width].reshape(held * ff, width)
+        own_ref[...] = jnp.dot(mixed_in, down, preferred_element_type=jnp.float32).reshape(n_expert, tok_rows, width)
+        ret_out_ref[c] = own_ref[...].astype(jnp.bfloat16)
+        for k in range(n_expert - 1):
+            ret_copy(c, k, peers[k], me).start()
+        ret_in_ref[c, me] = own_ref[me].astype(jnp.bfloat16)
+    for c in range(OUT_CHUNKS):
+        for k in range(n_expert - 1):
+            ret_copy(c, k, peers[k], peers[k]).wait_recv()
+        total = jnp.sum(ret_in_ref[c].astype(jnp.float32), axis=0)
+        out_ref[:, c * width:(c + 1) * width] = total.astype(jnp.bfloat16)
+
+    for k in range(n_expert - 1):
+        tok_copy(k, me).wait_send()
+        route_copy(k, me).wait_send()
+        for c in range(OUT_CHUNKS):
+            ret_copy(c, k, peers[k], me).wait_send()
+
+    def drain(i, carry):
+        for f in range(2):
+            @pl.when(far[f] < last)
+            def _():
+                rs_copy(f, i).wait_send()
+
+            @pl.when(far[f] > 0)
+            def _():
+                ag_copy(f, i).wait_send()
+
+        return carry
+
+    lax.fori_loop(0, items, drain, 0)
+
+
+def every_expert(tokens, w_gate, w_up, w_down, expert_ids, route_weights):
+    n_expert = lax.axis_size("expert")
+    n_tensor = lax.axis_size("tensor")
+    held, depth, ff = w_gate.shape
+    tok_rows, cols = tokens.shape
+    all_rows = n_expert * tok_rows
+    items = held * (ff // LANES) // 2
+    width = cols // OUT_CHUNKS
+    labels = jnp.arange(LANES, dtype=jnp.int32)
+    chosen = expert_ids[:, :, None] == labels[None, None, :]
+    routes = jnp.sum(jnp.where(chosen, route_weights[:, :, None], 0.0), axis=1)
+    dma = pltpu.SemaphoreType.DMA
+    vmem = pl.BlockSpec(memory_space=pltpu.VMEM)
+    hbm = pl.BlockSpec(memory_space=pl.ANY)
+    bf16 = jnp.bfloat16
+    return pl.pallas_call(
+        functools.partial(layer_kernel, n_expert, n_tensor),
+        out_shape=jax.ShapeDtypeStruct((tok_rows, cols), bf16),
+        in_specs=[vmem, vmem, hbm, hbm, hbm],
+        out_specs=vmem,
+        scratch_shapes=[
+            pltpu.VMEM((n_expert, tok_rows, cols), bf16),
+            pltpu.VMEM((n_expert, tok_rows, LANES), jnp.float32),
+            pltpu.VMEM((held, all_rows, LANES), jnp.float32),
+            pltpu.VMEM(w_gate.shape, bf16),
+            pltpu.VMEM(w_up.shape, bf16),
+            pltpu.VMEM(w_down.shape, bf16),
+            pltpu.VMEM((2, all_rows, 2 * LANES), jnp.float32),
+            pltpu.VMEM((2, items, all_rows, 2 * LANES), bf16),
+            pltpu.VMEM((2, items, all_rows, 2 * LANES), bf16),
+            pltpu.VMEM((2, items, all_rows, LANES), bf16),
+            pltpu.VMEM((n_expert, tok_rows, width), jnp.float32),
+            pltpu.VMEM((OUT_CHUNKS, n_expert, tok_rows, width), bf16),
+            pltpu.VMEM((OUT_CHUNKS, n_expert, tok_rows, width), bf16),
+            dma((2 * held + 1,)),
+            dma((n_expert - 1,)),
+            dma((n_expert,)),
+            dma((n_expert - 1,)),
+            dma((n_expert,)),
+            dma((2, items)),
+            dma((2, items)),
+            dma((2, items)),
+            dma((2, items)),
+            dma((OUT_CHUNKS, n_expert - 1)),
+            dma((OUT_CHUNKS, n_expert)),
+        ],
+        compiler_params=pltpu.CompilerParams(
+            collective_id=0, has_side_effects=True, vmem_limit_bytes=56 * 1024 * 1024
+        ),
+    )(tokens, routes, w_gate, w_up, w_down)
+
+
+def per_device(tokens, w_gate, w_up, w_down, expert_ids, route_weights):
+    experts_all = w_gate.shape[0] * lax.axis_size("expert")
+    if expert_ids.shape[1] == experts_all:
+        return every_expert(tokens, w_gate, w_up, w_down, expert_ids, route_weights)
+    return routed_by_slots(tokens, w_gate, w_up, w_down, expert_ids, route_weights)
+
+
 def solution(mesh):
     in_specs = (
         P(("group", "expert"), "tensor"),

time: 236 us -> 96 us (0.41)
  waiting for transfers between devices: 168 us -> 0 us
  Pallas kernels: 0 us -> 91.9 us
  blocking collectives: 18.5 us -> 0 us
  matrix products: 17.6 us -> 0 us
  between operations: 13.2 us -> 0.01 us
  local copies, waits for them, and re-layouts: 9.18 us -> 3.11 us
  other arithmetic: 5.83 us -> 0.82 us
  starting transfers between devices: 3.6 us -> 0 us
    reduce_scatter x2 -> x0, waiting for transfers between devices: 117 us -> none  [the longest x1 62.6 us: per_device(): lax.psum_scatter(up_part, 'tensor', scatter_dimension=3, tiled=True)]
    pallas_call x0 -> x1, Pallas kernels: none -> 91.9 us  [every_expert(): pl.pallas_call(functools.partial(layer_kernel, n_expert, n_tensor), out_s...]
    all_gather x1 -> x0, waiting for transfers between devices: 36.7 us -> none  [per_device(): hidden = lax.all_gather(hidden_share, 'tensor', axis=3, tiled=True)]
    all_to_all x1 -> x0, blocking collectives: 18.5 us -> none  [per_device(): lax.all_to_all(outgoing, 'expert', split_axis=0, concat_axis=0, tiled=True)]
    dot_general x3 -> x0, matrix products: 17.6 us -> none  [the longest x1 6.3 us: per_device(): jnp.einsum('sjnd,jdf->sjnf', received, w_up, preferred_element_type=jnp.f...]
    all_to_all x1 -> x0, waiting for transfers between devices: 14.3 us -> none  [per_device(): lax.all_to_all(returned, 'expert', split_axis=0, concat_axis=0, tiled=True)]
    gather x2 -> x0, local copies, waits for them, and re-layouts: 4.1 us -> none  [the longest x1 2.05 us: per_device(): tokens[jnp.maximum(source, 0)]]
    all_to_all x1 -> x0, starting transfers between devices: 3.51 us -> none  [per_device(): lax.all_to_all(returned, 'expert', split_axis=0, concat_axis=0, tiled=True)]
  transfers between devices with their start and end apart: 4 -> 0, of which waited for: 4 -> 0; matrix products, arithmetic and copies ran while one was open for 3% -> 0% of each run, Pallas kernels for 0% -> 0%
where the time goes in v1:
time: 96 us; the launch traced here: 95.8 us
  Pallas kernels  91.9 us (96%)
  local copies, waits for them, and re-layouts  3.11 us (3%)
    pallas_call x1, Pallas kernels, every_expert(): pl.pallas_call(functools.partial(layer_kernel, n_expert, n_tensor), out_s...  91.9 us
    unnamed x3, local copies, waits for them, and re-layouts  3.11 us

profile of v1, /device:TPU:0, one launch (start us, length us, event | category | flops | bytes accessed | tf_op | source)
XLA Modules:
  0.0 95.8 jit_solution(14849983917485142200)
XLA Ops:
  0.0 0.8 copy.9
  0.8 0.8 copy.10
  1.5 0.8 select_reduce_fusion.route_ref
  2.4 91.9 %shard_map.64 = bf16[64,1024]{1,0:T(8,128)(2,1)} custom-call(bf16[64,1024]{1,0:T(8,128)(2,1)} %tok_ref.1, f32[64,128]{1,0:T(8,128)} %select_reduce_fusion.route_ref, bf16[2,1024,1536]{2,1,0:T(8,128)(2,1)} %wg_hbm.1, bf16[2,1024,1536]{2,1,0:T(8,128)(2,1)} %wu_hbm.1, bf16[2,1536,1024]{2,1,0:T(8,128)(2,1)} %wd_hbm.1), custom_call_target="tpu_custom_call" | custom-call | tf_op jit(solution)/shard_map/pallas_call | solution.py:255
  94.2 1.6 %copy.12 = bf16[64,1024]{1,0:T(8,128)(2,1)} copy(bf16[64,1024]{1,0:T(8,128)(2,1)} %shard_map.64) | data formatting | bytes 262144

commit v2 on v1

--- a/solution.py
+++ b/solution.py
@@ -48,17 +48,18 @@
 
 
 LANES = 128
-RS_LAG = 2
-AG_LAG = 2
-OUT_CHUNKS = 4
+RS_LAG = 3
+AG_LAG = 3
+OUT_WIDTH = 256
 MESH = pl.DeviceIdType.MESH
 
 
 def layer_kernel(
-    n_expert, n_tensor, tok_ref, route_ref, wg_hbm, wu_hbm, wd_hbm, out_ref,
-    rows_ref, routes_ref, scale_ref, wg_ref, wu_ref, wd_ref, part_ref, sent_ref, got_ref, hidden_ref,
-    own_ref, ret_out_ref, ret_in_ref,
-    w_sem, tok_send, tok_recv, route_send, route_recv, rs_send, rs_recv, ag_send, ag_recv, ret_send, ret_recv,
+    n_expert, n_tensor, tok_ref, ids_ref, weights_ref, wg_hbm, wu_hbm, wd_hbm, out_ref,
+    rows_ref, route_ref, routes_ref, scale_ref, wg_ref, wu_ref, wd_ref, part_ref, sent_ref, got_ref, hidden_ref,
+    acc_ref, pair_ref, far_out_ref, far_in_ref,
+    w_sem, tok_send, tok_recv, pass_send, route_send, route_recv, rs_send, rs_recv, ag_send, ag_recv,
+    pair_send, pair_recv, home_send, home_recv,
 ):
     held, depth, ff = wg_ref.shape
     tok_rows, cols = tok_ref.shape
@@ -69,6 +70,12 @@
     at = lax.axis_index("tensor")
     last = n_tensor - 1
     peers = [lax.rem(me + k, n_expert) for k in range(1, n_expert)]
+    chips = n_expert // 2
+    core = lax.rem(me, 2)
+    chip = me // 2
+    partner = 2 * chip + 1 - core
+    same = [2 * lax.rem(chip + k, chips) + core for k in range(chips)]
+    other = [2 * lax.rem(chip + k, chips) + 1 - core for k in range(chips)]
 
     loads = []
     for j in range(held):
@@ -96,30 +103,37 @@
     def tok_copy(k, slot):
         return pltpu.make_async_remote_copy(
             src_ref=tok_ref, dst_ref=rows_ref.at[slot], send_sem=tok_send.at[k], recv_sem=tok_recv.at[slot],
-            device_id={"expert": peers[k]}, device_id_type=MESH)
+            device_id={"expert": same[k] if k else partner}, device_id_type=MESH)
+
+    def pass_copy(k, slot):
+        return pltpu.make_async_remote_copy(
+            src_ref=rows_ref.at[slot], dst_ref=rows_ref.at[slot], send_sem=pass_send.at[k],
+            recv_sem=tok_recv.at[slot], device_id={"expert": partner}, device_id_type=MESH)
 
     def route_copy(k, slot):
         return pltpu.make_async_remote_copy(
             src_ref=route_ref, dst_ref=routes_ref.at[slot], send_sem=route_send.at[k], recv_sem=route_recv.at[slot],
             device_id={"expert": peers[k]}, device_id_type=MESH)
 
-    for k in range(n_expert - 1):
+    for k in range(chips - 1, -1, -1):
         tok_copy(k, me).start()
+    rows_ref[me] = tok_ref[...]
+    labels = lax.broadcasted_iota(jnp.int32, (tok_rows, LANES), 1)
+    routes = jnp.zeros((tok_rows, LANES), jnp.float32)
+    for k in range(ids_ref.shape[1]):
+        routes += jnp.where(ids_ref[:, k:k + 1] == labels, weights_ref[:, k:k + 1], 0.0)
+    route_ref[...] = routes
+    routes_ref[me] = routes
+    for k in range(1, chips):
+        tok_copy(k, same[k]).wait_recv()
+        pass_copy(k, same[k]).start()
     for k in range(n_expert - 1):
         route_copy(k, me).start()
-    rows_ref[me] = tok_ref[...]
-    routes_ref[me] = route_ref[...]
     for load in loads[:-1]:
         load.wait()
-    for k in range(n_expert - 1):
-        tok_copy(k, peers[k]).wait_recv()
-    for k in range(n_expert - 1):
-        route_copy(k, peers[k]).wait_recv()
-    routes = routes_ref[...].reshape(all_rows, LANES)
-    lane = lax.broadcasted_iota(jnp.int32, (all_rows, LANES), 1)
-    for j in range(held):
-        mine = jnp.sum(jnp.where(lane == me * held + j, routes, 0.0), axis=1, keepdims=True)
-        scale_ref[j] = jnp.broadcast_to(mine, (all_rows, LANES))
+    tok_copy(0, partner).wait_recv()
+    for k in range(1, chips):
+        pass_copy(k, other[k]).wait_recv()
 
     far = (last - at, at)
     onward = (jnp.maximum(at - 1, 0), jnp.minimum(at + 1, last))
@@ -161,13 +175,6 @@
             hidden_ref[f, i] = (jax.nn.silu(gate) * up * scale_ref[j]).astype(jnp.bfloat16)
             ag_copy(f, i).start()
 
-    def forward(f, i):
-        ag_copy(f, i).wait_recv()
-
-        @pl.when(far[f] > 0)
-        def _():
-            ag_copy(f, i).start()
-
     def step(s, carry):
         for f in range(2):
             i = s - RS_LAG * far[f]
@@ -177,12 +184,6 @@
                 compute_part(f, i)
 
         for f in range(2):
-            h = s - RS_LAG * last - AG_LAG * (last - far[f])
-
-            @pl.when((h >= 0) & (h < items) & (far[f] < last))
-            def _():
-                forward(f, h)
-
             i = s - RS_LAG * far[f]
 
             @pl.when((i >= 0) & (i < items))
@@ -191,36 +192,75 @@
 
         return carry
 
-    lax.fori_loop(0, items + (RS_LAG + AG_LAG) * last, step, 0)
+    lax.fori_loop(0, RS_LAG * last, step, 0)
+
+    for k in range(n_expert - 1):
+        route_copy(k, peers[k]).wait_recv()
+    all_routes = routes_ref[...].reshape(all_rows, LANES)
+    lane = lax.broadcasted_iota(jnp.int32, (all_rows, LANES), 1)
+    for j in range(held):
+        mine = jnp.sum(jnp.where(lane == me * held + j, all_routes, 0.0), axis=1, keepdims=True)
+        scale_ref[j] = jnp.broadcast_to(mine, (all_rows, LANES))
+
+    lax.fori_loop(RS_LAG * last, items + RS_LAG * last, step, 0)
 
     loads[-1].wait()
-
-    def ret_copy(c, k, target, source):
-        return pltpu.make_async_remote_copy(
-            src_ref=ret_out_ref.at[c, target], dst_ref=ret_in_ref.at[c, source],
-            send_sem=ret_send.at[c, k], recv_sem=ret_recv.at[c, source],
-            device_id={"expert": peers[k]}, device_id_type=MESH)
-
-    width = cols // OUT_CHUNKS
-    mixed_in = jnp.concatenate([hidden_ref[f, i] for f in range(2) for i in range(items)], axis=1)
-    for c in range(OUT_CHUNKS):
-        down = wd_ref[:, :, c * width:(c + 1) * width].reshape(held * ff, width)
-        own_ref[...] = jnp.dot(mixed_in, down, preferred_element_type=jnp.float32).reshape(n_expert, tok_rows, width)
-        ret_out_ref[c] = own_ref[...].astype(jnp.bfloat16)
-        for k in range(n_expert - 1):
-            ret_copy(c, k, peers[k], me).start()
-        ret_in_ref[c, me] = own_ref[me].astype(jnp.bfloat16)
-    for c in range(OUT_CHUNKS):
-        for k in range(n_expert - 1):
-            ret_copy(c, k, peers[k], peers[k]).wait_recv()
-        total = jnp.sum(ret_in_ref[c].astype(jnp.float32), axis=0)
-        out_ref[:, c * width:(c + 1) * width] = total.astype(jnp.bfloat16)
-
+    acc_ref[...] = jnp.zeros_like(acc_ref)
+
+    def collect(s, carry):
+        for f in range(2):
+            i = s - AG_LAG * (last - far[f])
+
+            @pl.when((i >= 0) & (i < items) & (far[f] < last))
+            def _():
+                ag_copy(f, i).wait_recv()
+
+                @pl.when(far[f] > 0)
+                def _():
+                    ag_copy(f, i).start()
+
+        for f in range(2):
+            i = s - AG_LAG * (last - far[f])
+
+            @pl.when((i >= 0) & (i < items) & (lax.rem(i + items, 2) == 1))
+            def _():
+                q = f * items + i - 1
+                j = q // per_expert
+                start = pl.multiple_of(lax.rem(q, per_expert) * LANES, LANES)
+                pair = jnp.concatenate([hidden_ref[f, i - 1], hidden_ref[f, i]], axis=1)
+                for c in range(0, cols, OUT_WIDTH):
+                    down = wd_ref[j, pl.ds(start, 2 * LANES), c:c + OUT_WIDTH]
+                    term = jnp.dot(pair, down, preferred_element_type=jnp.float32)
+                    acc_ref[:, :, c:c + OUT_WIDTH] += term.reshape(n_expert, tok_rows, OUT_WIDTH)
+
+        return carry
+
+    lax.fori_loop(0, items + AG_LAG * last, collect, 0)
+
+    def pair_copy(k):
+        return pltpu.make_async_remote_copy(
+            src_ref=acc_ref.at[other[k]], dst_ref=pair_ref.at[k], send_sem=pair_send.at[k],
+            recv_sem=pair_recv.at[k], device_id={"expert": partner}, device_id_type=MESH)
+
+    def home_copy(k):
+        return pltpu.make_async_remote_copy(
+            src_ref=far_out_ref.at[k], dst_ref=far_in_ref.at[k], send_sem=home_send.at[k],
+            recv_sem=home_recv.at[k], device_id={"expert": same[k]}, device_id_type=MESH)
+
+    for k in range(chips - 1, -1, -1):
+        pair_copy(k).start()
+    for k in range(1, chips):
+        pair_copy(k).wait_recv()
+        far_out_ref[k] = (acc_ref[same[k]] + pair_ref[k]).astype(jnp.bfloat16)
+        home_copy(k).start()
+
+    for k in range(chips):
+        tok_copy(k, me).wait_send()
+        pair_copy(k).wait_send()
+        if k:
+            pass_copy(k, same[k]).wait_send()
     for k in range(n_expert - 1):
-        tok_copy(k, me).wait_send()
         route_copy(k, me).wait_send()
-        for c in range(OUT_CHUNKS):
-            ret_copy(c, k, peers[k], me).wait_send()
 
     def drain(i, carry):
         for f in range(2):
@@ -235,6 +275,16 @@
         return carry
 
     lax.fori_loop(0, items, drain, 0)
+
+    pair_copy(0).wait_recv()
+    acc_ref[me] += pair_ref[0]
+    total = acc_ref[me]
+    for k in range(1, chips):
+        home_copy(k).wait_recv()
+        total = total + far_in_ref[k].astype(jnp.float32)
+    out_ref[...] = total.astype(jnp.bfloat16)
+    for k in range(1, chips):
+        home_copy(k).wait_send()
 
 
 def every_expert(tokens, w_gate, w_up, w_down, expert_ids, route_weights):
@@ -244,10 +294,7 @@
     tok_rows, cols = tokens.shape
     all_rows = n_expert * tok_rows
     items = held * (ff // LANES) // 2
-    width = cols // OUT_CHUNKS
-    labels = jnp.arange(LANES, dtype=jnp.int32)
-    chosen = expert_ids[:, :, None] == labels[None, None, :]
-    routes = jnp.sum(jnp.where(chosen, route_weights[:, :, None], 0.0), axis=1)
+    chips = n_expert // 2
     dma = pltpu.SemaphoreType.DMA
     vmem = pl.BlockSpec(memory_space=pltpu.VMEM)
     hbm = pl.BlockSpec(memory_space=pl.ANY)
@@ -255,10 +302,11 @@
     return pl.pallas_call(
         functools.partial(layer_kernel, n_expert, n_tensor),
         out_shape=jax.ShapeDtypeStruct((tok_rows, cols), bf16),
-        in_specs=[vmem, vmem, hbm, hbm, hbm],
+        in_specs=[vmem, vmem, vmem, hbm, hbm, hbm],
         out_specs=vmem,
         scratch_shapes=[
             pltpu.VMEM((n_expert, tok_rows, cols), bf16),
+            pltpu.VMEM((tok_rows, LANES), jnp.float32),
             pltpu.VMEM((n_expert, tok_rows, LANES), jnp.float32),
             pltpu.VMEM((held, all_rows, LANES), jnp.float32),
             pltpu.VMEM(w_gate.shape, bf16),
@@ -268,25 +316,29 @@
             pltpu.VMEM((2, items, all_rows, 2 * LANES), bf16),
             pltpu.VMEM((2, items, all_rows, 2 * LANES), bf16),
             pltpu.VMEM((2, items, all_rows, LANES), bf16),
-            pltpu.VMEM((n_expert, tok_rows, width), jnp.float32),
-            pltpu.VMEM((OUT_CHUNKS, n_expert, tok_rows, width), bf16),
-            pltpu.VMEM((OUT_CHUNKS, n_expert, tok_rows, width), bf16),
+            pltpu.VMEM((n_expert, tok_rows, cols), jnp.float32),
+            pltpu.VMEM((chips, tok_rows, cols), jnp.float32),
+            pltpu.VMEM((chips, tok_rows, cols), bf16),
+            pltpu.VMEM((chips, tok_rows, cols), bf16),
             dma((2 * held + 1,)),
-            dma((n_expert - 1,)),
+            dma((chips,)),
             dma((n_expert,)),
+            dma((chips,)),
             dma((n_expert - 1,)),
             dma((n_expert,)),
             dma((2, items)),
             dma((2, items)),
             dma((2, items)),
             dma((2, items)),
-            dma((OUT_CHUNKS, n_expert - 1)),
-            dma((OUT_CHUNKS, n_expert)),
+            dma((chips,)),
+            dma((chips,)),
+            dma((chips,)),
+            dma((chips,)),
         ],
         compiler_params=pltpu.CompilerParams(
             collective_id=0, has_side_effects=True, vmem_limit_bytes=56 * 1024 * 1024
         ),
-    )(tokens, routes, w_gate, w_up, w_down)
+    )(tokens, expert_ids, route_weights, w_gate, w_up, w_down)
 
 
 def per_device(tokens, w_gate, w_up, w_down, expert_ids, route_weights):

time: 96 us -> 90.3 us (0.941); the launches traced: 95.8 us -> 88.8 us
  Pallas kernels: 91.9 us -> 84.4 us
  local copies, waits for them, and re-layouts: 3.11 us -> 4.32 us
    pallas_call x1, Pallas kernels: 91.9 us -> 84.4 us  [every_expert(): pl.pallas_call(functools.partial(layer_kernel, n_expert, n_tensor), out_s...]
    unnamed x3, local copies, waits for them, and re-layouts: 3.11 us -> 4.32 us
where the time goes in v2:
time: 90.3 us; the launch traced here: 88.8 us
  Pallas kernels  84.4 us (93%)
  local copies, waits for them, and re-layouts  4.32 us (5%)
    pallas_call x1, Pallas kernels, every_expert(): pl.pallas_call(functools.partial(layer_kernel, n_expert, n_tensor), out_s...  84.4 us
    unnamed x3, local copies, waits for them, and re-layouts  4.32 us

profile of v2, /device:TPU:0, one launch (start us, length us, event | category | flops | bytes accessed | tf_op | source)
XLA Modules:
  0.0 88.8 jit_solution(12987218615558665671)
XLA Ops:
  0.0 1.4 %copy.7.ids_ref = s32[64,8]{1,0:T(8,128)} copy(s32[64,8]{0,1:T(8,128)} %param.10) | data formatting | bytes 4096 | tf_op args[4]
  1.4 1.4 %copy.8.weights_ref = f32[64,8]{1,0:T(8,128)} copy(f32[64,8]{0,1:T(8,128)} %param.11) | data formatting | bytes 4096 | tf_op args[5]
  2.8 84.4 %shard_map.64 = bf16[64,1024]{1,0:T(8,128)(2,1)} custom-call(bf16[64,1024]{1,0:T(8,128)(2,1)} %tok_ref.1, s32[64,8]{1,0:T(8,128)} %copy.7.ids_ref, f32[64,8]{1,0:T(8,128)} %copy.8.weights_ref, bf16[2,1024,1536]{2,1,0:T(8,128)(2,1)} %wg_hbm.1, bf16[2,1024,1536]{2,1,0:T(8,128)(2,1)} %wu_hbm.1, bf16[2,1536,1024]{2,1,0:T(8,128)(2,1)} %wd_hbm.1), custom_call_target="tpu_custom_call" | custom-call | tf_op jit(solution)/shard_map/pallas_call | solution.py:302
  87.2 1.6 %copy.10 = bf16[64,1024]{1,0:T(8,128)(2,1)} copy(bf16[64,1024]{1,0:T(8,128)(2,1)} %shard_map.64) | data formatting | bytes 262144

commit v3 on v2

--- a/solution.py
+++ b/solution.py
@@ -118,15 +118,15 @@
     for k in range(chips - 1, -1, -1):
         tok_copy(k, me).start()
     rows_ref[me] = tok_ref[...]
+    for k in range(1, chips):
+        tok_copy(k, same[k]).wait_recv()
+        pass_copy(k, same[k]).start()
     labels = lax.broadcasted_iota(jnp.int32, (tok_rows, LANES), 1)
     routes = jnp.zeros((tok_rows, LANES), jnp.float32)
     for k in range(ids_ref.shape[1]):
         routes += jnp.where(ids_ref[:, k:k + 1] == labels, weights_ref[:, k:k + 1], 0.0)
     route_ref[...] = routes
     routes_ref[me] = routes
-    for k in range(1, chips):
-        tok_copy(k, same[k]).wait_recv()
-        pass_copy(k, same[k]).start()
     for k in range(n_expert - 1):
         route_copy(k, me).start()
     for load in loads[:-1]:

time: 90.3 us -> 90.3 us (level)
  no operation moved by 1% of the time
where the time goes in v3:
time: 90.3 us; the launch traced here: 88.8 us
  Pallas kernels  84.4 us (93%)
  local copies, waits for them, and re-layouts  4.32 us (5%)
    pallas_call x1, Pallas kernels, every_expert(): pl.pallas_call(functools.partial(layer_kernel, n_expert, n_tensor), out_s...  84.4 us
    unnamed x3, local copies, waits for them, and re-layouts  4.32 us

profile of v3, /device:TPU:0, one launch (start us, length us, event | category | flops | bytes accessed | tf_op | source)
XLA Modules:
  0.0 88.8 jit_solution(13050417230825859825)
XLA Ops:
  0.0 1.4 %copy.7.ids_ref = s32[64,8]{1,0:T(8,128)} copy(s32[64,8]{0,1:T(8,128)} %param.10) | data formatting | bytes 4096 | tf_op args[4]
  1.4 1.4 %copy.8.weights_ref = f32[64,8]{1,0:T(8,128)} copy(f32[64,8]{0,1:T(8,128)} %param.11) | data formatting | bytes 4096 | tf_op args[5]
  2.8 84.4 %shard_map.64 = bf16[64,1024]{1,0:T(8,128)(2,1)} custom-call(bf16[64,1024]{1,0:T(8,128)(2,1)} %tok_ref.1, s32[64,8]{1,0:T(8,128)} %copy.7.ids_ref, f32[64,8]{1,0:T(8,128)} %copy.8.weights_ref, bf16[2,1024,1536]{2,1,0:T(8,128)(2,1)} %wg_hbm.1, bf16[2,1024,1536]{2,1,0:T(8,128)(2,1)} %wu_hbm.1, bf16[2,1536,1024]{2,1,0:T(8,128)(2,1)} %wd_hbm.1), custom_call_target="tpu_custom_call" | custom-call | tf_op jit(solution)/shard_map/pallas_call | solution.py:302
  87.2 1.6 %copy.10 = bf16[64,1024]{1,0:T(8,128)(2,1)} copy(bf16[64,1024]{1,0:T(8,128)(2,1)} %shard_map.64) | data formatting | bytes 262144
